TPU v7x, 512 devices: a whole 4x4x16 slice. The times are simulated.
512 devices in a mesh: ctx: 64 (over z, y_hi, core), req: 8 (over y_lo, x).
Axes of the slice: x: 4, y: 4 (y_hi: 2, y_lo: 2; y = y_hi * 2 + y_lo), z: 16, core: 2. Of those that a mesh axis runs over, the one named last changes fastest.
Arguments:
- hidden: bfloat16 [1024, 5120], P('req'), parts along dimension 0, may hold values from -6 to 6
- w_query: bfloat16 [5120, 8192], P(None, 'ctx'), may hold values from -0.078125 to 0.078125
- key_projection_weight: bfloat16 [5120, 1024], P(None, 'ctx'), may hold values from -0.078125 to 0.078125
- value_projection_weight: bfloat16 [5120, 1024], P(None, 'ctx'), may hold values from -0.078125 to 0.078125
- query_gain: float32 [128], replicated, may hold values from 0.5 to 1.5
- key_gain: float32 [128], replicated, may hold values from 4 to 8
- stored_cache_keys: bfloat16 [65536, 1024], P(('req', 'ctx')), parts along dimension 0, may hold values from -100 to 100
- stored_cache_values: bfloat16 [65536, 1024], P(('req', 'ctx')), parts along dimension 0, may hold values from -8 to 8
- cache_length: int32 [8], P('req'), parts along dimension 0, may hold values from 4096 to 8192
- first_position: int32 [8], P('req'), parts along dimension 0, may hold values from 0 to 4095
Outputs:
- attended: bfloat16 [1024, 8192], P('req', 'ctx'), parts along dimension 0
There are 8 independent parts, one for each index of `req`. A program takes and returns all parts, laid end to end along the dimension named above; an argument that names none is the same for every part. Nothing has to cross between parts.
All inputs are finite; a program needn't handle non-finite values.
Results may differ from a plain program's by a relative error of at most 0.013.
The roundings to bfloat16 on the way count: a program that leaves them out, or rounds other values in their place, can miss the bound.
Values may be sent and summed in bfloat16 or wider, within the bound.
No kernel may reach another device: no remote copies, remote signals or barrier semaphores. Data moves between devices by JAX's collectives and lax.ppermute only.
A program may use at most 128 MiB of HBM per device.

v0:
```python
import math

import jax
import jax.numpy as jnp
from jax import lax
from jax.sharding import Mesh
from jax.sharding import PartitionSpec as P

CTX = ("ctx_0", "ctx_1", "ctx_2")
REQ_CTX = ("req", "ctx_0", "ctx_1", "ctx_2")


def gather_turned(arrays, axis, dims):
    turned = [jnp.moveaxis(a, dim, 0) for a, dim in zip(arrays, dims)]
    widths = [t[0].size for t in turned]
    both = jnp.concatenate([t.reshape(-1, w) for t, w in zip(turned, widths)], axis=1)
    filled = lax.all_gather(both, axis, axis=0, tiled=True)
    pieces = jnp.split(filled, [sum(widths[:k]) for k in range(1, len(widths))], axis=1)
    return tuple(
        (
            jnp.moveaxis(b.reshape(-1, *t.shape[1:]), 0, dim)
            for b, t, dim in zip(pieces, turned, dims)
        )
    )


def laid_out(pieces, dim):
    shape = list(pieces.shape[1:])
    shape[dim] *= pieces.shape[0]
    return jnp.moveaxis(pieces, 0, dim).reshape(shape)


def gather_in_order(value, axes, turns):
    pieces = value
    for k in turns:
        pieces = lax.all_gather(pieces, axes[k])
    done = turns[::-1]
    back = [done.index(k) for k in range(len(axes))]
    pieces = pieces.transpose(*back, *range(len(axes), pieces.ndim))
    return pieces.reshape(-1, *value.shape)


def gather_axes(value, axes, turns, dim):
    return laid_out(gather_in_order(value, axes, turns), dim)


def sent_together(arrays, axis, split_dim, concat_dim, along):
    columns = [a.reshape(*a.shape[:along], -1) for a in arrays]
    both = jnp.concatenate(columns, axis=along)
    filled, at, outs = (
        lax.all_to_all(both, axis, split_axis=split_dim, concat_axis=concat_dim, tiled=True),
        0,
        [],
    )
    for a, column in zip(arrays, columns):
        section = filled[..., at : at + column.shape[along]]
        outs.append(section.reshape(*section.shape[:along], *a.shape[along:]))
        at += column.shape[along]
    return tuple(outs)


def normalize(joined_values, gain):
    mean_square = jnp.mean(joined_values * joined_values, axis=-1, keepdims=True)
    return joined_values * lax.rsqrt(mean_square + 1e-06) * gain


def rotate(joined_values, positions):
    half = joined_values.shape[-1] // 2
    freq = jnp.exp(
        jnp.arange(half, dtype=jnp.float32) * (-2.0 * math.log(1000000.0) / joined_values.shape[-1])
    )
    angles = positions[:, None] * freq[None, :]
    cosine = jnp.concatenate([jnp.cos(angles), jnp.cos(angles)], axis=-1)[:, None, :]
    sine = jnp.concatenate([jnp.sin(angles), jnp.sin(angles)], axis=-1)[:, None, :]
    turned = jnp.concatenate([-joined_values[..., half:], joined_values[..., :half]], axis=-1)
    return joined_values * cosine + turned * sine


def soft_weights(scores, visible):
    masked = jnp.where(visible, scores, -1e30)
    top = jnp.max(masked, axis=-1)
    weights = jnp.where(visible, jnp.exp(masked - top[..., None]), 0.0)
    return (weights, top, jnp.sum(weights, axis=-1))


def join(first, second):
    top = jnp.maximum(first[1], second[1])
    scale_a = jnp.exp(first[1] - top)
    scale_b = jnp.exp(second[1] - top)
    summed = first[0] * scale_a[..., None] + second[0] * scale_b[..., None]
    return (summed, top, first[2] * scale_a + second[2] * scale_b)


def fold_sources(received):
    sums, maxima, totals = received
    top = jnp.max(maxima, axis=1)
    factor = jnp.exp(maxima - top[:, None])
    return (jnp.sum(sums * factor[..., None], axis=1), top, jnp.sum(totals * factor, axis=1))


def per_device(
    hidden,
    w_query,
    key_projection_weight,
    value_projection_weight,
    query_gain,
    key_gain,
    stored_cache_keys,
    stored_cache_values,
    cache_length,
    first_position,
):
    groups = lax.axis_size(CTX)
    rank = lax.axis_index(CTX)
    input_tokens = hidden.shape[0]
    head_dim = query_gain.shape[0]
    heads_here = w_query.shape[1] // head_dim
    all_heads = heads_here * groups
    kv_heads = stored_cache_keys.shape[1] // head_dim
    query_group = all_heads // kv_heads
    slots = stored_cache_keys.shape[0]
    scale = 1.0 / math.sqrt(head_dim)
    positions = first_position[0].astype(jnp.float32) + jnp.arange(input_tokens, dtype=jnp.float32)
    projected = jnp.dot(hidden, w_query, preferred_element_type=jnp.float32).reshape(
        input_tokens, heads_here, head_dim
    )
    own_queries = (
        rotate(normalize(projected, query_gain), positions).astype(jnp.bfloat16).transpose(1, 0, 2)
    )
    key_part = jnp.dot(hidden, key_projection_weight, preferred_element_type=jnp.float32).astype(
        jnp.bfloat16
    )
    value_part = jnp.dot(
        hidden, value_projection_weight, preferred_element_type=jnp.float32
    ).astype(jnp.bfloat16)
    key_full, value_full = gather_turned((key_part, value_part), CTX, (1, 1))
    key_float = (
        key_full.astype(jnp.float32).reshape(input_tokens, head_dim, kv_heads).transpose(0, 2, 1)
    )
    incoming_keys = rotate(normalize(key_float, key_gain), positions).astype(jnp.bfloat16)
    incoming_values = value_full.reshape(input_tokens, head_dim, kv_heads).transpose(0, 2, 1)
    query_states = gather_axes(own_queries, CTX, (1, 0, 2), 0)
    token_rows = query_states.reshape(kv_heads, query_group * input_tokens, head_dim)
    valid = (rank * slots + jnp.arange(slots, dtype=jnp.int32) < cache_length[0])[None, :]

    def shard_term(index):
        query_rows = lax.dynamic_index_in_dim(token_rows, index, 0, keepdims=False)
        key_rows = lax.dynamic_slice_in_dim(stored_cache_keys, index * head_dim, head_dim, 1)
        value_rows = lax.dynamic_slice_in_dim(stored_cache_values, index * head_dim, head_dim, 1)
        scores = (
            lax.dot_general(
                query_rows, key_rows, (((1,), (1,)), ((), ())), preferred_element_type=jnp.float32
            )
            * scale
        )
        weights, top, total = soft_weights(scores, valid)
        summed = jnp.dot(
            weights.astype(jnp.bfloat16), value_rows, preferred_element_type=jnp.float32
        )
        return (summed, top, total)

    sums, maxima, totals = lax.map(shard_term, jnp.arange(kv_heads, dtype=jnp.int32))
    sums = sums.reshape(all_heads, input_tokens, head_dim)
    maxima = maxima.reshape(all_heads, input_tokens)
    totals = totals.reshape(all_heads, input_tokens)
    received = sent_together((sums[:, None], maxima[:, None], totals[:, None]), CTX, 0, 1, 3)
    merged = fold_sources(received)
    head_ids = rank * heads_here + jnp.arange(heads_here, dtype=jnp.int32)
    chosen = head_ids // query_group
    keys_here = jnp.take(incoming_keys, chosen, axis=1)
    values_here = jnp.take(incoming_values, chosen, axis=1)
    scores = (
        jnp.einsum("htd,shd->hts", own_queries, keys_here, preferred_element_type=jnp.float32)
        * scale
    )
    causal = (jnp.arange(input_tokens)[None, :] <= jnp.arange(input_tokens)[:, None])[None]
    weights, top, total = soft_weights(scores, causal)
    fresh = jnp.einsum(
        "hts,shd->htd",
        weights.astype(jnp.bfloat16),
        values_here,
        preferred_element_type=jnp.float32,
    )
    final = join((fresh, top, total), merged)
    attention_output = final[0] / final[2][..., None]
    return (
        attention_output.transpose(1, 0, 2)
        .reshape(input_tokens, heads_here * head_dim)
        .astype(jnp.bfloat16)
    )


def solution(mesh):
    finer = Mesh(
        mesh.devices.reshape(16, 2, 2, mesh.shape["req"]), ("ctx_0", "ctx_1", "ctx_2", "req")
    )
    return jax.shard_map(
        per_device,
        mesh=finer,
        in_specs=(
            P("req", None),
            P(None, CTX),
            P(None, CTX),
            P(None, CTX),
            P(),
            P(),
            P(REQ_CTX, None),
            P(REQ_CTX, None),
            P("req"),
            P("req"),
        ),
        out_specs=P("req", CTX),
        check_vma=False,
    )
```

profile of v0, /device:TPU:1, one launch (start us, length us, event | category | flops | bytes accessed | tf_op | source)
XLA Modules:
  0.0 499.5 jit_solution(5183464044391376757)
XLA Ops:
  6.5 1.3 copy-done
  7.9 2.0 multiply_reduce_fusion.1
  11.4 1.3 pad_maximum_fusion.1
  12.7 5.7 %all-gather = bf16[256,128]{0,1:T(8,128)(2,1)S(1)} all-gather(bf16[128,128]{0,1:T(8,128)(2,1)S(1)} %get-tuple-element.125), channel_id=2, replica_groups=mesh['ctx_0'=16,'ctx_1'=2,'ctx_2'=2,'req'=8] {'ctx_1'}, dimensions={0}, use_global_device_ids=true | all-gather | bytes 98304 | tf_op jit(solution)/shard_map/all_gather | solution.py:36
  19.2 66.1 %all-gather.6.cloned.1.call-done = bf16[32,1,128,128]{3,2,1,0:T(8,128)(2,1)} async-done(((bf16[2,1,128,128]{3,2,1,0:T(8,128)(2,1)}), bf16[32,1,128,128]{3,2,1,0:T(8,128)(2,1)}) %all-gather.6.cloned.1.call-update) | async-done | bytes 1048592 | tf_op jit(solution)/shard_map/all_gather | solution.py:36
  85.4 31.9 %all-gather.8.cloned.1.call-done = bf16[32,2,1,128,128]{4,3,2,1,0:T(8,128)(2,1)} async-done(((bf16[16,2,1,128,128]{4,3,2,1,0:T(8,128)(2,1)}), bf16[32,2,1,128,128]{4,3,2,1,0:T(8,128)(2,1)}) %all-gather.8.cloned.1.call-update) | async-done | bytes 2097168 | tf_op jit(solution)/shard_map/all_gather | solution.py:36
  117.3 1.7 copy.64
  119.1 69.1 %while.16 = (s32[]{:T(128)}, f32[8,1024,128]{2,1,0:T(8,128)}, f32[8,1024]{1,0:T(8,128)S(1)}, f32[8,1024]{1,0:T(8,128)}, s32[8]{0:T(128)S(1)}, /*index=5*/bf16[8,...) while((s32[]{:T(128)}, f32[8,1024,128]{2,1,0:T(8,128)}, ...), condition=%wide.region_6.8_spmd.clone, body=%wide.region_3.7_spmd.clone.sunk | while | flops 68286728 | bytes 2459269 | solution.py:162
  124.2 1.9 fusion.76
  126.2 1.4 dynamic_update_slice.20
  132.8 2.0 fusion.76
  134.9 1.4 dynamic_update_slice.20
  141.5 1.9 fusion.76
  143.6 1.4 dynamic_update_slice.20
  149.1 1.0 fusion.75
  150.2 1.9 fusion.76
  152.2 1.4 dynamic_update_slice.20
  158.8 1.9 fusion.76
  160.8 1.4 dynamic_update_slice.20
  167.4 1.9 fusion.76
  169.4 1.4 dynamic_update_slice.20
  176.0 1.9 fusion.76
  178.1 1.4 dynamic_update_slice.20
  184.7 1.9 fusion.76
  186.7 1.4 dynamic_update_slice.20
  188.2 6.0 %reshape_broadcast_in_dim_reshape.8 = f32[64,1,128,1]{3,2,0,1:T(8,128)} reshape(f32[8,1024]{1,0:T(8,128)S(1)} %get-tuple-element.56) | data formatting | bytes 65536 | tf_op jit(solution)/shard_map/reshape;broadcast_in_dim;reshape | solution.py:48
  194.2 6.1 %reshape_broadcast_in_dim_reshape.9 = f32[64,1,128,1]{3,2,0,1:T(8,128)} reshape(f32[8,1024]{1,0:T(8,128)S(1)} %copy-done.4) | data formatting | bytes 65536 | tf_op jit(solution)/shard_map/reshape;broadcast_in_dim;reshape | solution.py:48
  200.3 7.6 %pad_maximum_fusion = f32[64,1,128,130]{3,2,0,1:T(8,128)} fusion(f32[64,1,128,1]{3,2,0,1:T(8,128)} %reshape_broadcast_in_dim_reshape.9, f32[64,1,128,1]{3,2,0,1:T(8,128)} %reshape_broadcast_in_dim_reshape.8, f32[64,1,128,128]{3,2,0,1:T(8,128)} %bitcast.98), kind=kLoop, calls=%fused_computation.19 | loop fusion | flops 2129920 | bytes 8519680 | tf_op jit(solution)/shard_map/concatenate | solution.py:49
  207.9 12.4 %copy.67 = f32[64,1,128,130]{2,1,3,0:T(1,128)} copy(f32[64,1,128,130]{3,2,0,1:T(8,128)} %pad_maximum_fusion) | data formatting | bytes 8519680 | tf_op jit(solution)/shard_map/concatenate | solution.py:49
  220.2 14.7 %all-to-all-start = ((f32[64,1,128,130]{2,1,3,0:T(1,128)}), f32[64,1,128,130]{2,1,3,0:T(1,128)}, u32[]{:S(2)}, u32[]{:S(2)}) async-start(f32[64,1,128,130]{2,1,3,0:T(1,128)} %copy.67), calls=%async_computation | async-start | bytes 8519680 | tf_op jit(solution)/shard_map/all_to_all | solution.py:51
  236.1 250.6 %all_gather.18 = bf16[1024,256]{1,0:T(8,128)(2,1)S(1)} all-gather(bf16[16,256]{1,0:T(8,128)(2,1)S(1)} %pad_maximum_fusion.3), channel_id=1, replica_groups=mesh['ctx_0'=16,'ctx_1'=2,'ctx_2'=2,'req'=8] {'ctx_0','ctx_1','ctx_2'}, dimensions={0}, use_global_device_ids=true | all-gather | bytes 532480 | tf_op jit(solution)/shard_map/all_gather | solution.py:17
  488.1 2.8 copy.72
  (87 shorter events, 25.1 us)
Async XLA Ops:
  6.5 1.3 copy-start
  6.5 78.8 %all-gather.6.cloned.1.call-start = ((), (), s32[]{:S(2)}) async-start(), calls=%async_computation.1 | async-start | bytes 1114112 | tf_op jit(solution)/shard_map/all_gather | solution.py:36
  19.2 98.1 %all-gather.8.cloned.1.call-start = ((), (), s32[]{:S(2)}) async-start(), calls=%async_computation.2 | async-start | bytes 3145728 | tf_op jit(solution)/shard_map/all_gather | solution.py:36
  188.2 6.1 %copy-start.4 = (f32[8,1024]{1,0:T(8,128)S(1)}, f32[8,1024]{1,0:T(8,128)}, u32[]{:S(2)}) copy-start(f32[8,1024]{1,0:T(8,128)} %get-tuple-element.57) | copy-start | bytes 98308
  220.2 14.8 %copy-start.1 = (f32[128,128]{0,1:T(8,128)S(1)}, f32[128,128]{0,1:T(8,128)}, u32[]{:S(2)}) copy-start(f32[128,128]{0,1:T(8,128)} %get-tuple-element.124) | copy-start | bytes 196612
  220.2 15.0 %copy-start.2 = (bf16[5120,16]{0,1:T(8,128)(2,1)S(1)}, bf16[5120,16]{0,1:T(8,128)(2,1)}, u32[]{:S(2)}) copy-start(bf16[5120,16]{0,1:T(8,128)(2,1)} %param.17) | copy-start | bytes 491524
  220.2 15.4 %copy-start.3 = (bf16[5120,16]{0,1:T(8,128)(2,1)S(1)}, bf16[5120,16]{0,1:T(8,128)(2,1)}, u32[]{:S(2)}) copy-start(bf16[5120,16]{0,1:T(8,128)(2,1)} %param.16) | copy-start | bytes 491524
  220.2 267.9 %all-to-all-start = ((f32[64,1,128,130]{2,1,3,0:T(1,128)}), f32[64,1,128,130]{2,1,3,0:T(1,128)}, u32[]{:S(2)}, u32[]{:S(2)}) async-start(f32[64,1,128,130]{2,1,3,0:T(1,128)} %copy.67), calls=%async_computation | async-start | bytes 8519680 | tf_op jit(solution)/shard_map/all_to_all | solution.py:51
  235.0 252.5 %copy-start.5 = (f32[128]{0:T(128)S(1)}, f32[128]{0:T(128)}, u32[]{:S(2)}) copy-start(f32[128]{0:T(128)} %param.19) | copy-start | bytes 1540
Sparse Core Ops, SparseCore 0:
  19.3 66.0 all-gather.5
  87.5 29.8 all-gather.7
where the time goes:
time: 502 us; the launch traced here: 500 us
  blocking collectives  256 us (51%)
  waiting for transfers between devices  98 us (20%)
  local copies, waits for them, and re-layouts  48.9 us (10%)
  matrix products  27.3 us (5%)
  loops' own time  22.5 us (4%)
  other arithmetic  17.5 us (3%)
  starting transfers between devices  14.8 us (3%)
  between operations  14.3 us (3%)
    all_gather x1, blocking collectives, gather_turned(): filled = lax.all_gather(both, axis, axis=0, tiled=True)  251 us
    all_gather x2, waiting for transfers between devices, gather_in_order(): pieces = lax.all_gather(pieces, axes[k])  98 us
    another operation x1, loops' own time, per_device(): lax.map(shard_term, jnp.arange(kv_heads, dtype=jnp.int32))  22.5 us
    dot_general x8, matrix products, shard_term(): jnp.dot(weights.astype(jnp.bfloat16), value_rows, preferred_element_type=...  15.3 us
    all_to_all x1, starting transfers between devices, sent_together(): lax.all_to_all(both, axis, split_axis=split_dim, concat_axis=concat_dim,...  14.7 us
    concatenate x1, local copies, waits for them, and re-layouts, sent_together(): both = jnp.concatenate(columns, axis=along)  12.4 us
    another operation x2, local copies, waits for them, and re-layouts, sent_together(): columns = [a.reshape(*a.shape[:along], -1) for a in arrays]  12.1 us
    dynamic_update_slice x16, local copies, waits for them, and re-layouts, per_device(): lax.map(shard_term, jnp.arange(kv_heads, dtype=jnp.int32))  11.7 us
  transfers between devices with their start and end apart: 3, of which 2 were waited for; matrix products, arithmetic and copies ran while one was open for 0% of the time, Pallas kernels for 0%

commit v1 on v0

v1 whole, which is shorter than its diff:
```python
import math

import jax
import jax.numpy as jnp
from jax import lax
from jax.experimental import pallas as pl
from jax.experimental.pallas import tpu as pltpu
from jax.sharding import Mesh
from jax.sharding import PartitionSpec as P

FAR = "far"
NEAR = ("near_z", "near_y", "core")
CTX = (FAR, *NEAR)
REQ_CTX = ("req", *CTX)

HIDDEN_MASK = -1e30
STAT_ROWS = 16


def normalize_columns(values, gain):
    mean_square = jnp.mean(values * values, axis=0, keepdims=True)
    return values * lax.rsqrt(mean_square + 1e-06) * gain[:, None]


def rotate_columns(values, cosine, sine):
    half = values.shape[0] // 2
    turned = jnp.concatenate([-values[half:], values[:half]], axis=0)
    return values * cosine + turned * sine


def angles_of(first_position, tokens, head_dim):
    half = head_dim // 2
    positions = first_position[0].astype(jnp.float32) + jnp.arange(tokens, dtype=jnp.float32)
    freq = jnp.exp(
        jnp.arange(half, dtype=jnp.float32) * (-2.0 * math.log(1000000.0) / head_dim)
    )
    angles = freq[:, None] * positions[None, :]
    cosine = jnp.cos(angles)
    sine = jnp.sin(angles)
    return (
        jnp.concatenate([cosine, cosine], axis=0),
        jnp.concatenate([sine, sine], axis=0),
    )


def shard_kernel(limit_ref, queries_ref, cache_ref, out_ref, values_ref, scores_ref):
    heads, head_dim, tokens = queries_ref.shape
    shards, _, slots, _ = cache_ref.shape
    scale = 1.0 / math.sqrt(head_dim)
    limit = limit_ref[0]
    near = limit_ref[1]
    for shard in range(shards):
        values_ref[:, shard * slots : (shard + 1) * slots] = cache_ref[shard, 1].T
    slot = lax.broadcasted_iota(jnp.int32, (slots, tokens), 0)

    def one_head(head, carry):
        query = queries_ref[head]
        top = jnp.full((1, tokens), HIDDEN_MASK, jnp.float32)
        for shard in range(shards):
            scores = (
                jnp.dot(cache_ref[shard, 0], query, preferred_element_type=jnp.float32) * scale
            )
            visible = slot < limit - (shard * 8 + near) * slots
            scores = jnp.where(visible, scores, HIDDEN_MASK)
            scores_ref[shard * slots : (shard + 1) * slots, :] = scores
            top = jnp.maximum(top, jnp.max(scores, axis=0, keepdims=True))
        top = top.astype(jnp.bfloat16).astype(jnp.float32)
        scores = scores_ref[...]
        weights = jnp.where(scores > 0.5 * HIDDEN_MASK, jnp.exp(scores - top), 0.0)
        total = jnp.sum(weights, axis=0, keepdims=True)
        summed = jnp.dot(
            values_ref[...], weights.astype(jnp.bfloat16), preferred_element_type=jnp.float32
        )
        high = total.astype(jnp.bfloat16).astype(jnp.float32)
        row = lax.broadcasted_iota(jnp.int32, (STAT_ROWS, tokens), 0)
        stats = jnp.where(row == 0, top, jnp.where(row == 1, high, total - high))
        out_ref[head, :head_dim, :] = summed.astype(jnp.bfloat16)
        out_ref[head, head_dim:, :] = stats.astype(jnp.bfloat16)
        return carry

    lax.fori_loop(0, heads, one_head, 0)


def final_kernel(query_ref, keys_ref, values_ref, received_ref, out_ref):
    head_dim, tokens = query_ref.shape
    sources = received_ref.shape[0]
    scale = 1.0 / math.sqrt(head_dim)
    scores = (
        lax.dot_general(
            keys_ref[...],
            query_ref[...],
            (((0,), (0,)), ((), ())),
            preferred_element_type=jnp.float32,
        )
        * scale
    )
    source = lax.broadcasted_iota(jnp.int32, (tokens, tokens), 0)
    token = lax.broadcasted_iota(jnp.int32, (tokens, tokens), 1)
    causal = source <= token
    scores = jnp.where(causal, scores, HIDDEN_MASK)
    top = jnp.max(scores, axis=0, keepdims=True)
    stats = [
        received_ref[k, head_dim : head_dim + STAT_ROWS, :].astype(jnp.float32)
        for k in range(sources)
    ]
    for k in range(sources):
        top = jnp.maximum(top, stats[k][0:1])
    weights = jnp.where(causal, jnp.exp(scores - top), 0.0)
    total = jnp.sum(weights, axis=0, keepdims=True)
    summed = jnp.dot(
        values_ref[...], weights.astype(jnp.bfloat16), preferred_element_type=jnp.float32
    )
    for k in range(sources):
        factor = jnp.exp(stats[k][0:1] - top)
        total = total + factor * (stats[k][1:2] + stats[k][2:3])
        summed = summed + factor * received_ref[k, :head_dim, :].astype(jnp.float32)
    out_ref[...] = (summed / total).T.astype(jnp.bfloat16)


def per_device(
    hidden,
    w_query,
    key_projection_weight,
    value_projection_weight,
    query_gain,
    key_gain,
    stored_cache_keys,
    stored_cache_values,
    cache_length,
    first_position,
):
    tokens = hidden.shape[0]
    head_dim = query_gain.shape[0]
    slots = stored_cache_keys.shape[0]
    kv_heads = stored_cache_keys.shape[1] // head_dim
    near = lax.axis_index(NEAR)
    near_size = lax.axis_size(NEAR)
    far_size = lax.axis_size(FAR)

    cache = jnp.stack(
        [
            stored_cache_keys.reshape(slots, kv_heads, head_dim).transpose(1, 0, 2),
            stored_cache_values.reshape(slots, kv_heads, head_dim).transpose(1, 0, 2),
        ],
        axis=1,
    )
    cache = lax.all_to_all(cache, FAR, 0, 0, tiled=True)

    weights = (((0,), (1,)), ((), ()))
    key_part = lax.dot_general(
        key_projection_weight, hidden, weights, preferred_element_type=jnp.float32
    ).astype(jnp.bfloat16)
    value_part = lax.dot_general(
        value_projection_weight, hidden, weights, preferred_element_type=jnp.float32
    ).astype(jnp.bfloat16)
    part = jnp.stack([key_part, value_part]).reshape(2, -1, kv_heads, tokens)
    entries = part.shape[1]
    part = part.transpose(2, 0, 1, 3).reshape(kv_heads, 2 * entries, tokens)
    part = lax.all_to_all(part, FAR, 0, 0, tiled=True)

    cosine, sine = angles_of(first_position, tokens, head_dim)
    projected = lax.dot_general(w_query, hidden, weights, preferred_element_type=jnp.float32)
    own_query = rotate_columns(normalize_columns(projected, query_gain), cosine, sine).astype(
        jnp.bfloat16
    )
    both = jnp.concatenate([own_query, part.reshape(-1, tokens)], axis=0)
    gathered = lax.all_gather(both, NEAR)
    queries = gathered[:, :head_dim]
    fresh = gathered[:, head_dim:].reshape(near_size, far_size, 2, entries, tokens)
    fresh = fresh.transpose(2, 1, 0, 3, 4).reshape(2, head_dim, tokens)
    new_keys = rotate_columns(
        normalize_columns(fresh[0].astype(jnp.float32), key_gain), cosine, sine
    ).astype(jnp.bfloat16)
    new_values = fresh[1]

    limits = jnp.stack([cache_length[0], near.astype(jnp.int32)])
    partial = pl.pallas_call(
        shard_kernel,
        out_shape=jax.ShapeDtypeStruct(
            (near_size, head_dim + STAT_ROWS, tokens), jnp.bfloat16
        ),
        in_specs=[
            pl.BlockSpec(memory_space=pltpu.SMEM),
            pl.BlockSpec(memory_space=pltpu.VMEM),
            pl.BlockSpec(memory_space=pltpu.VMEM),
        ],
        out_specs=pl.BlockSpec(memory_space=pltpu.VMEM),
        scratch_shapes=[
            pltpu.VMEM((head_dim, far_size * slots), jnp.bfloat16),
            pltpu.VMEM((far_size * slots, tokens), jnp.float32),
        ],
        cost_estimate=pl.CostEstimate(
            flops=4 * near_size * tokens * head_dim * far_size * slots,
            bytes_accessed=1 << 20,
            transcendentals=near_size * tokens * far_size * slots,
        ),
        name="cache_term",
    )(limits, queries, cache)
    received = lax.all_to_all(partial, NEAR, 0, 0, tiled=True)
    return pl.pallas_call(
        final_kernel,
        out_shape=jax.ShapeDtypeStruct((tokens, head_dim), jnp.bfloat16),
        name="final_join",
    )(own_query, new_keys, new_values, received)


def solution(mesh):
    finer = Mesh(
        mesh.devices.reshape(8, 2, 2, 2, mesh.shape["req"]),
        (*CTX, "req"),
    )
    return jax.shard_map(
        per_device,
        mesh=finer,
        in_specs=(
            P("req", None),
            P(None, CTX),
            P(None, CTX),
            P(None, CTX),
            P(),
            P(),
            P(REQ_CTX, None),
            P(REQ_CTX, None),
            P("req"),
            P("req"),
        ),
        out_specs=P("req", CTX),
        check_vma=False,
    )
```

time: 502 us -> 89.9 us (0.18)
  blocking collectives: 256 us -> 30.9 us
  waiting for transfers between devices: 98 us -> 14.9 us
  local copies, waits for them, and re-layouts: 48.9 us -> 5.02 us
  matrix products: 27.3 us -> 2.35 us
  loops' own time: 22.5 us -> 0 us
  other arithmetic: 17.5 us -> 3.37 us
  between operations: 14.3 us -> 1.46 us
  starting transfers between devices: 14.8 us -> 23.3 us
  Pallas kernels: 0 us -> 8.18 us
    all_gather x2 -> x1, blocking collectives: 256 us -> 30.9 us  [per_device(): gathered = lax.all_gather(both, NEAR)]
    all_gather x2 -> x0, waiting for transfers between devices: 98 us -> none  [gather_in_order(): pieces = lax.all_gather(pieces, axes[k])]
    dot_general x21 -> x3, matrix products: 27.3 us -> 2.35 us  [the longest x1 1.35 us: per_device(): lax.dot_general(key_projection_weight, hidden, weights, preferred_element...]
    another operation x1 -> x0, loops' own time: 22.5 us -> none  [per_device(): lax.map(shard_term, jnp.arange(kv_heads, dtype=jnp.int32))]
    all_to_all x1 -> x3, waiting for transfers between devices: 0.01 us -> 14.9 us  [the longest x1 9.79 us: per_device(): part = lax.all_to_all(part, FAR, 0, 0, tiled=True)]
    concatenate x3 -> x0, local copies, waits for them, and re-layouts: 12.5 us -> none  [the longest x1 12.4 us: sent_together(): both = jnp.concatenate(columns, axis=along)]
    another operation x2 -> x0, local copies, waits for them, and re-layouts: 12.1 us -> none  [sent_together(): columns = [a.reshape(*a.shape[:along], -1) for a in arrays]]
    dynamic_update_slice x16 -> x0, local copies, waits for them, and re-layouts: 11.7 us -> none  [per_device(): lax.map(shard_term, jnp.arange(kv_heads, dtype=jnp.int32))]
  transfers between devices with their start and end apart: 3 -> 3, of which waited for: 2 -> 2; matrix products, arithmetic and copies ran while one was open for 0% -> 6% of each run, Pallas kernels for 0% -> 0%
where the time goes in v1:
time: 89.9 us; the launch traced here: 89.4 us
  blocking collectives  30.9 us (34%)
  starting transfers between devices  23.3 us (26%)
  waiting for transfers between devices  14.9 us (17%)
  Pallas kernels  8.18 us (9%)
  local copies, waits for them, and re-layouts  5.02 us (6%)
  other arithmetic  3.37 us (4%)
  matrix products  2.35 us (3%)
  between operations  1.46 us (2%)
    all_gather x1, blocking collectives, per_device(): gathered = lax.all_gather(both, NEAR)  30.9 us
    all_to_all x1, starting transfers between devices, per_device(): part = lax.all_to_all(part, FAR, 0, 0, tiled=True)  15.6 us
    all_to_all x1, waiting for transfers between devices, per_device(): part = lax.all_to_all(part, FAR, 0, 0, tiled=True)  9.79 us
    pallas_call x1, Pallas kernels, per_device(): pl.pallas_call(shard_kernel, out_shape=jax.ShapeDtypeStruct((near_size, h...  6.08 us
    all_to_all x1, waiting for transfers between devices, per_device(): received = lax.all_to_all(partial, NEAR, 0, 0, tiled=True)  5.09 us
    all_to_all x1, starting transfers between devices, per_device(): received = lax.all_to_all(partial, NEAR, 0, 0, tiled=True)  4.15 us
    all_to_all x1, starting transfers between devices, per_device(): cache = lax.all_to_all(cache, FAR, 0, 0, tiled=True)  3.49 us
    unnamed x22, local copies, waits for them, and re-layouts  3.26 us
  transfers between devices with their start and end apart: 3, of which 2 were waited for; matrix products, arithmetic and copies ran while one was open for 6% of the time, Pallas kernels for 0%

profile of v1, /device:TPU:1, one launch (start us, length us, event | category | flops | bytes accessed | tf_op | source)
XLA Modules:
  0.0 89.4 jit_solution(8935077565539783450)
XLA Ops:
  0.0 1.3 %copy-done = bf16[128,5120]{1,0:T(8,128)(2,1)S(1)} copy-done((bf16[128,5120]{1,0:T(8,128)(2,1)S(1)}, bf16[128,5120]{1,0:T(8,128)(2,1)}, u32[]{:S(2)}) %copy-start) | copy-done | bytes 1310744
  1.3 1.3 %fusion = bf16[1,2,8,128]{3,2,1,0:T(8,128)(2,1)S(1)} fusion(bf16[5120,16]{0,1:T(8,128)(2,1)} %param.12, bf16[128,5120]{1,0:T(8,128)(2,1)S(1)} %copy-done), kind=kOutput, calls=%fused_computation.2 | convolution fusion | flops 20973568 | bytes 1478656 | tf_op jit(solution)/shard_map/dot_general | solution.py:150
  2.7 0.5 fusion.1
  3.1 0.6 copy.13
  3.8 15.6 %all-to-all-start = ((bf16[8,4,128]{2,1,0:T(4,128)(2,1)}), bf16[8,4,128]{2,1,0:T(4,128)(2,1)S(1)}, u32[]{:S(2)}, u32[]{:S(2)}) async-start(bf16[8,4,128]{2,1,0:T(4,128)(2,1)} %bitcast.4), calls=%async_computation | async-start | bytes 16384 | tf_op jit(solution)/shard_map/all_to_all | solution.py:159
  19.4 0.2 copy.15
  19.6 0.2 copy.16
  19.8 0.2 copy.17
  19.9 0.0 copy-start.1
  20.0 0.2 copy.18
  20.1 0.8 pad_maximum_fusion
  21.0 9.8 %all-to-all-done = bf16[8,4,128]{2,1,0:T(4,128)(2,1)S(1)} async-done(((bf16[8,4,128]{2,1,0:T(4,128)(2,1)}), bf16[8,4,128]{2,1,0:T(4,128)(2,1)S(1)}, u32[]{:S(2)}, u32[]{:S(2)}) %all-to-all-start) | async-done | bytes 8224 | tf_op jit(solution)/shard_map/all_to_all | solution.py:159
  30.8 3.5 %all-to-all-start.1 = ((bf16[8,2,128,128]{3,2,1,0:T(8,128)(2,1)}), bf16[8,2,128,128]{3,2,1,0:T(8,128)(2,1)S(1)}, u32[]{:S(2)}, u32[]{:S(2)}) async-start(bf16[8,2,128,128]{3,2,1,0:T(8,128)(2,1)} %pad_maximum_fusion), calls=%async_computation.1 | async-start | bytes 1048576 | tf_op jit(solution)/shard_map/all_to_all | solution.py:147
  35.6 0.6 pad_add_fusion.limit_ref
  36.2 0.5 multiply_reduce_fusion.1
  36.8 0.1 copy-done.8
  36.9 0.1 multiply_multiply_fusion.1
  36.9 0.2 multiply_sine_fusion
  37.1 0.1 fusion.5.query_ref
  37.3 30.9 %all-gather = bf16[1280,128]{1,0:T(8,128)(2,1)S(1)} all-gather(bf16[160,128]{1,0:T(8,128)(2,1)S(1)} %pad_maximum_fusion.3), channel_id=2, replica_groups=mesh['far'=8,'near_z'=2,'near_y'=2,'core'=2,'req'=8] {'near_z','near_y',..., dimensions={0}, use_global_device_ids=true | all-gather | bytes 368640 | tf_op jit(solution)/shard_map/all_gather | solution.py:167
  68.2 0.7 slice.41.queries_ref
  68.9 0.1 multiply_reduce_fusion
  69.0 0.0 all-to-all-done.1.cache_ref
  69.0 0.8 copy-done.3
  69.8 6.1 %cache_term.1 = bf16[8,144,128]{2,1,0:T(8,128)(2,1)} custom-call(s32[2]{0:T(128)} %pad_add_fusion.limit_ref, bf16[8,128,128]{2,1,0:T(8,128)(2,1)} %slice.41.queries_ref, bf16[8,2,128,128]{3,2,1,0:T(8,128)(2,1)} %copy-done.3), custom_call_target="tpu_custom_call" | custom-call | flops 536870912 | bytes 1048576 | tf_op jit(solution)/shard_map/cache_term/pallas_call | solution.py:177
  75.9 4.1 %all-to-all-start.2 = ((bf16[8,144,128]{2,1,0:T(8,128)(2,1)}), bf16[8,144,128]{2,1,0:T(8,128)(2,1)S(1)}, u32[]{:S(2)}, u32[]{:S(2)}) async-start(bf16[8,144,128]{2,1,0:T(8,128)(2,1)} %cache_term.1), calls=%async_computation.2 | async-start | bytes 589824 | tf_op jit(solution)/shard_map/all_to_all | solution.py:199
  80.1 0.7 fusion.9
  80.7 0.1 multiply_multiply_fusion
  80.8 0.7 fusion.7.keys_ref
  81.5 5.1 %all-to-all-done.2.received_ref = bf16[8,144,128]{2,1,0:T(8,128)(2,1)S(1)} async-done(((bf16[8,144,128]{2,1,0:T(8,128)(2,1)}), bf16[8,144,128]{2,1,0:T(8,128)(2,1)S(1)}, u32[]{:S(2)}, u32[]{:S(2)}) %all-to-all-start.2) | async-done | bytes 294944 | tf_op jit(solution)/shard_map/all_to_all | solution.py:199
  86.6 0.7 copy-done.2
  87.3 2.1 %final_join.1 = bf16[128,128]{1,0:T(8,128)(2,1)} custom-call(bf16[128,128]{1,0:T(8,128)(2,1)} %copy-done.4, bf16[128,128]{1,0:T(8,128)(2,1)} %fusion.7.keys_ref, bf16[128,128]{1,0:T(8,128)(2,1)} %bitcast.42, bf16[8,144,128]{2,1,0:T(8,128)(2,1)} %copy-done.2), custom_call_target="tpu_custom_call" | custom-call | tf_op jit(solution)/shard_map/final_join/pallas_call | solution.py:200
  (24 shorter events, 0.1 us)
Async XLA Ops:
  0.0 1.3 %copy-start = (bf16[128,5120]{1,0:T(8,128)(2,1)S(1)}, bf16[128,5120]{1,0:T(8,128)(2,1)}, u32[]{:S(2)}) copy-start(bf16[128,5120]{1,0:T(8,128)(2,1)} %param.10) | copy-start | bytes 3932164
  0.0 2.7 %copy-start.7 = (bf16[5120,16]{0,1:T(8,128)(2,1)S(1)}, bf16[5120,16]{0,1:T(8,128)(2,1)}, u32[]{:S(2)}) copy-start(bf16[5120,16]{0,1:T(8,128)(2,1)} %param.13) | copy-start | bytes 491524
  0.0 19.4 %copy-start.5 = (bf16[128,1024]{1,0:T(8,128)(2,1)S(1)}, bf16[128,1024]{1,0:T(8,128)(2,1)}, u32[]{:S(2)}) copy-start(bf16[128,1024]{1,0:T(8,128)(2,1)} %param.16) | copy-start | bytes 786436
  2.7 17.1 %copy-start.6 = (bf16[128,1024]{1,0:T(8,128)(2,1)S(1)}, bf16[128,1024]{1,0:T(8,128)(2,1)}, u32[]{:S(2)}) copy-start(bf16[128,1024]{1,0:T(8,128)(2,1)} %param.17) | copy-start | bytes 786436
  3.8 27.0 %all-to-all-start = ((bf16[8,4,128]{2,1,0:T(4,128)(2,1)}), bf16[8,4,128]{2,1,0:T(4,128)(2,1)S(1)}, u32[]{:S(2)}, u32[]{:S(2)}) async-start(bf16[8,4,128]{2,1,0:T(4,128)(2,1)} %bitcast.4), calls=%async_computation | async-start | bytes 16384 | tf_op jit(solution)/shard_map/all_to_all | solution.py:159
  19.9 16.3 %copy-start.1 = (bf16[5120,128]{1,0:T(8,128)(2,1)S(1)}, bf16[5120,128]{1,0:T(8,128)(2,1)}, u32[]{:S(2)}) copy-start(bf16[5120,128]{1,0:T(8,128)(2,1)} %param.11) | copy-start | bytes 3932164
  30.8 38.2 %all-to-all-start.1 = ((bf16[8,2,128,128]{3,2,1,0:T(8,128)(2,1)}), bf16[8,2,128,128]{3,2,1,0:T(8,128)(2,1)S(1)}, u32[]{:S(2)}, u32[]{:S(2)}) async-start(bf16[8,2,128,128]{3,2,1,0:T(8,128)(2,1)} %pad_maximum_fusion), calls=%async_computation.1 | async-start | bytes 1048576 | tf_op jit(solution)/shard_map/all_to_all | solution.py:147
  36.2 0.7 copy-start.8
  37.2 38.7 %copy-start.4 = (bf16[128,128]{1,0:T(8,128)(2,1)}, bf16[128,128]{1,0:T(8,128)(2,1)S(1)}, u32[]{:S(2)}) copy-start(bf16[128,128]{1,0:T(8,128)(2,1)S(1)} %fusion.5.query_ref) | copy-start | bytes 98308
  69.0 11.7 %copy-start.9 = (f32[128]{0:T(128)S(1)}, f32[128]{0:T(128)}, u32[]{:S(2)}) copy-start(f32[128]{0:T(128)} %param.15) | copy-start | bytes 1540
  69.0 0.8 copy-start.3
  75.9 10.7 %all-to-all-start.2 = ((bf16[8,144,128]{2,1,0:T(8,128)(2,1)}), bf16[8,144,128]{2,1,0:T(8,128)(2,1)S(1)}, u32[]{:S(2)}, u32[]{:S(2)}) async-start(bf16[8,144,128]{2,1,0:T(8,128)(2,1)} %cache_term.1), calls=%async_computation.2 | async-start | bytes 589824 | tf_op jit(solution)/shard_map/all_to_all | solution.py:199
  86.6 0.7 copy-start.2

commit v2 on v1

v2 whole, which is shorter than its diff:
```python
import math

import jax
import jax.numpy as jnp
from jax import lax
from jax.experimental import pallas as pl
from jax.experimental.pallas import tpu as pltpu
from jax.sharding import PartitionSpec as P

FARS = 8
LOWS = 4
LINE = 2 * LOWS
NEVER = -1e30
FLOOR = -1e29
PART_ROWS = 8
STAT_ROWS = 8


def side_of(lane, far):
    return lane ^ 1 if far < FARS // 2 else lane


def rank_of(far, lane, low):
    return far * LINE + side_of(lane, far) * LOWS + low


LINES = [
    [rank_of(far, lane, low) for far in range(FARS)] for lane in range(2) for low in range(LOWS)
]
NEARS = [
    [rank_of(far, lane, low) for lane in range(2) for low in range(LOWS)] for far in range(FARS)
]
CORE_PAIRS = [[r, r + 1] for r in range(FARS * LINE) if r % 2 == 0]
ROW_PAIRS = [[r, r + 2] for r in range(FARS * LINE) if r // 2 % 2 == 0]
LANE_PAIRS = [
    [rank_of(far, lane, low) for lane in range(2)] for far in range(FARS) for low in range(LOWS)
]

WHOLE = pltpu.CompilerParams(vmem_limit_bytes=67043328)
SMALL = pltpu.CompilerParams(vmem_limit_bytes=24 << 20)
VMEM = pl.BlockSpec(memory_space=pltpu.VMEM)
HBM = pl.BlockSpec(memory_space=pltpu.HBM)
SMEM = pl.BlockSpec(memory_space=pltpu.SMEM)


def pack_kernel(
    hidden_hbm,
    key_weight_hbm,
    value_weight_hbm,
    keys_hbm,
    values_hbm,
    out_hbm,
    hidden_ref,
    key_weight_ref,
    value_weight_ref,
    keys_ref,
    values_ref,
    part_ref,
    in_sems,
    key_sems,
    value_sems,
    part_sems,
):
    slots = keys_ref.shape[0]
    head_dim = keys_ref.shape[1] // FARS
    loads = [
        pltpu.make_async_copy(source, target, in_sems.at[k])
        for k, (source, target) in enumerate(
            (
                (keys_hbm, keys_ref),
                (values_hbm, values_ref),
                (hidden_hbm, hidden_ref),
                (key_weight_hbm, key_weight_ref),
                (value_weight_hbm, value_weight_ref),
            )
        )
    ]
    for load in loads:
        load.start()
    stores = []
    for k, (ref, sems) in enumerate(((keys_ref, key_sems), (values_ref, value_sems))):
        loads[k].wait()
        for far in range(FARS):
            store = pltpu.make_async_copy(
                ref.at[:, pl.ds(far * head_dim, head_dim)],
                out_hbm.at[far, pl.ds(k * slots, slots), :],
                sems.at[far],
            )
            store.start()
            stores.append(store)
    for load in loads[2:]:
        load.wait()
    across = (((1,), (1,)), ((), ()))
    key_part, value_part = [
        lax.dot_general(ref[...], hidden_ref[...], across, preferred_element_type=jnp.float32)
        for ref in (key_weight_ref, value_weight_ref)
    ]
    entries = key_part.shape[0] // FARS
    rows = jnp.concatenate([key_part, value_part], axis=0)
    target = lax.broadcasted_iota(jnp.int32, (FARS * PART_ROWS, rows.shape[0]), 0)
    source = lax.broadcasted_iota(jnp.int32, (FARS * PART_ROWS, rows.shape[0]), 1)
    inside = target % PART_ROWS
    pick = (inside < 2 * entries) & (source == inside * FARS + target // PART_ROWS)
    ordered = jnp.dot(
        pick.astype(jnp.bfloat16), rows.astype(jnp.bfloat16), preferred_element_type=jnp.float32
    ).astype(jnp.bfloat16)
    for far in range(FARS):
        part_ref[far] = ordered[far * PART_ROWS : (far + 1) * PART_ROWS]
        store = pltpu.make_async_copy(
            part_ref.at[far], out_hbm.at[far, pl.ds(2 * slots, PART_ROWS), :], part_sems.at[far]
        )
        store.start()
        stores.append(store)
    for store in stores:
        store.wait()


def cache_kernel(limit_ref, queries_ref, cache_ref, out_ref, turned_ref, scores_ref, weights_ref):
    heads, head_dim, tokens = queries_ref.shape
    slots = (cache_ref.shape[1] - PART_ROWS) // 2
    factor = math.log2(math.e) / math.sqrt(head_dim)
    pairs = heads // 2
    wide = 2 * tokens
    for far in range(FARS):
        turned_ref[:, far * slots : (far + 1) * slots] = cache_ref[far, slots : 2 * slots].T
    slot = lax.broadcasted_iota(jnp.int32, (slots, wide), 0)

    rows = jnp.concatenate([cache_ref[far, 2 * slots :] for far in range(FARS)], axis=0)
    entries = head_dim // (FARS * LINE)
    kept = 2 * entries * FARS
    target = lax.broadcasted_iota(jnp.int32, (kept, FARS * PART_ROWS), 0)
    source = lax.broadcasted_iota(jnp.int32, (kept, FARS * PART_ROWS), 1)
    kind, place = target // (entries * FARS), target % (entries * FARS)
    wanted = (place // entries) * PART_ROWS + kind * entries + place % entries
    part = jnp.dot(
        (source == wanted).astype(jnp.bfloat16), rows, preferred_element_type=jnp.float32
    ).astype(jnp.bfloat16)
    for head in range(heads):
        out_ref[head, head_dim : head_dim + kept, :] = part

    def score(pair):
        query = jnp.concatenate([queries_ref[2 * pair], queries_ref[2 * pair + 1]], axis=1)
        top = jnp.full((1, wide), FLOOR, jnp.float32)
        for far in range(FARS):
            scores = jnp.dot(cache_ref[far, :slots], query, preferred_element_type=jnp.float32)
            scores = jnp.where(slot < limit_ref[far], scores, NEVER)
            scores_ref[pair, far * slots : (far + 1) * slots, :] = scores
            top = jnp.maximum(top, jnp.max(scores, axis=0, keepdims=True))
        return top.astype(jnp.bfloat16).astype(jnp.float32)

    def mix(pair, top):
        total = jnp.zeros((1, wide), jnp.float32)
        for far in range(FARS):
            block = slice(far * slots, (far + 1) * slots)
            weights = jnp.exp2((scores_ref[pair, block, :] - top) * factor)
            total = total + jnp.sum(weights, axis=0, keepdims=True)
            weights_ref[pair, block, :] = weights.astype(jnp.bfloat16)
        summed = jnp.dot(turned_ref[...], weights_ref[pair], preferred_element_type=jnp.float32)
        high = total.astype(jnp.bfloat16).astype(jnp.float32)
        row = lax.broadcasted_iota(jnp.int32, (STAT_ROWS, wide), 0)
        stats = jnp.where(row == 0, top, jnp.where(row == 1, high, total - high))
        for half in range(2):
            columns = slice(half * tokens, (half + 1) * tokens)
            out_ref[2 * pair + half, :head_dim, :] = summed[:, columns].astype(jnp.bfloat16)
            out_ref[2 * pair + half, head_dim + kept :, :] = stats[:, columns].astype(jnp.bfloat16)

    top = score(0)
    for pair in range(pairs):
        following = score(pair + 1) if pair + 1 < pairs else None
        mix(pair, top)
        top = following


def final_kernel(query_ref, received_ref, gain_ref, cosine_ref, sine_ref, out_ref):
    head_dim, tokens = query_ref.shape
    factor = math.log2(math.e) / math.sqrt(head_dim)
    entries = head_dim // (FARS * LINE)
    span = entries * FARS
    entry = lax.broadcasted_iota(jnp.int32, (head_dim, head_dim), 0)
    place = lax.broadcasted_iota(jnp.int32, (head_dim, head_dim), 1)
    lane, low = place // (span * LOWS), place // span % LOWS
    far = place % span // entries
    side = jnp.where(far < FARS // 2, 1 - lane, lane)
    wanted = ((far * 2 + side) * LOWS + low) * entries + place % entries
    pick = (entry == wanted).astype(jnp.bfloat16)

    def gathered(kind):
        first = head_dim + kind * span
        rows = jnp.concatenate([received_ref[k, first : first + span] for k in range(LINE)], axis=0)
        return jnp.dot(pick, rows, preferred_element_type=jnp.float32)

    raw = gathered(0)
    mean_square = jnp.mean(raw * raw, axis=0, keepdims=True)
    normed = raw * lax.rsqrt(mean_square + 1e-06) * gain_ref[...]
    half = head_dim // 2
    turned = jnp.concatenate([-normed[half:], normed[:half]], axis=0)
    new_keys = (normed * cosine_ref[...] + turned * sine_ref[...]).astype(jnp.bfloat16)
    new_values = gathered(1).astype(jnp.bfloat16)
    scores = jnp.dot(new_keys.T, query_ref[...], preferred_element_type=jnp.float32)
    source = lax.broadcasted_iota(jnp.int32, (tokens, tokens), 0)
    token = lax.broadcasted_iota(jnp.int32, (tokens, tokens), 1)
    scores = jnp.where(source <= token, scores, NEVER)
    top = jnp.max(scores, axis=0, keepdims=True)
    first = head_dim + 2 * span
    stats = [received_ref[k, first : first + STAT_ROWS].astype(jnp.float32) for k in range(LINE)]
    for k in range(LINE):
        top = jnp.maximum(top, stats[k][0:1])
    weights = jnp.exp2((scores - top) * factor)
    total = jnp.sum(weights, axis=0, keepdims=True)
    summed = jnp.dot(new_values, weights.astype(jnp.bfloat16), preferred_element_type=jnp.float32)
    for k in range(LINE):
        share = jnp.exp2((stats[k][0:1] - top) * factor)
        total = total + share * (stats[k][1:2] + stats[k][2:3])
        summed = summed + share * received_ref[k, :head_dim].astype(jnp.float32)
    out_ref[...] = (summed / total).T.astype(jnp.bfloat16)


def angles_of(first_position, tokens, head_dim):
    half = head_dim // 2
    positions = first_position[0].astype(jnp.float32) + jnp.arange(tokens, dtype=jnp.float32)
    freq = jnp.exp(jnp.arange(half, dtype=jnp.float32) * (-2.0 * math.log(1000000.0) / head_dim))
    angles = freq[:, None] * positions[None, :]
    cosine, sine = jnp.cos(angles), jnp.sin(angles)
    return jnp.concatenate([cosine, cosine], axis=0), jnp.concatenate([sine, sine], axis=0)


def query_kernel(hidden_ref, weight_ref, gain_ref, cosine_ref, sine_ref, own_ref):
    projected = jnp.dot(hidden_ref[...], weight_ref[...], preferred_element_type=jnp.float32)
    mean_square = jnp.mean(projected * projected, axis=1, keepdims=True)
    normed = (projected * lax.rsqrt(mean_square + 1e-06) * gain_ref[...]).T
    half = normed.shape[0] // 2
    turned = jnp.concatenate([-normed[half:], normed[:half]], axis=0)
    own_ref[...] = (normed * cosine_ref[...] + turned * sine_ref[...]).astype(jnp.bfloat16)


def per_device(
    hidden,
    w_query,
    key_projection_weight,
    value_projection_weight,
    query_gain,
    key_gain,
    stored_cache_keys,
    stored_cache_values,
    cache_length,
    first_position,
):
    tokens = hidden.shape[0]
    head_dim = query_gain.shape[0]
    slots = stored_cache_keys.shape[0]
    entries = key_projection_weight.shape[1] // FARS
    rank = lax.axis_index("ctx")

    packed = pl.pallas_call(
        pack_kernel,
        out_shape=jax.ShapeDtypeStruct((FARS, 2 * slots + PART_ROWS, head_dim), jnp.bfloat16),
        in_specs=[HBM] * 5,
        out_specs=HBM,
        scratch_shapes=[
            pltpu.VMEM(hidden.shape, jnp.bfloat16),
            pltpu.VMEM(key_projection_weight.shape[::-1], jnp.bfloat16),
            pltpu.VMEM(value_projection_weight.shape[::-1], jnp.bfloat16),
            pltpu.VMEM(stored_cache_keys.shape, jnp.bfloat16),
            pltpu.VMEM(stored_cache_values.shape, jnp.bfloat16),
            pltpu.VMEM((FARS, PART_ROWS, tokens), jnp.bfloat16),
            pltpu.SemaphoreType.DMA((5,)),
            pltpu.SemaphoreType.DMA((FARS,)),
            pltpu.SemaphoreType.DMA((FARS,)),
            pltpu.SemaphoreType.DMA((FARS,)),
        ],
        compiler_params=WHOLE,
        cost_estimate=pl.CostEstimate(flops=1 << 26, bytes_accessed=1 << 22, transcendentals=0),
        name="pack",
    )(
        hidden,
        key_projection_weight.T,
        value_projection_weight.T,
        stored_cache_keys,
        stored_cache_values,
    )
    cache = lax.all_to_all(packed, "ctx", 0, 0, axis_index_groups=LINES, tiled=True)

    cosine, sine = angles_of(first_position, tokens, head_dim)
    own_query = pl.pallas_call(
        query_kernel,
        out_shape=jax.ShapeDtypeStruct((head_dim, tokens), jnp.bfloat16),
        in_specs=[VMEM] * 5,
        out_specs=VMEM,
        compiler_params=SMALL,
        cost_estimate=pl.CostEstimate(flops=1 << 28, bytes_accessed=1 << 21, transcendentals=0),
        name="query",
    )(hidden, w_query, query_gain[None], cosine, sine)
    queries = own_query[None]
    for pairs in (CORE_PAIRS, ROW_PAIRS, LANE_PAIRS):
        queries = lax.all_gather(queries, "ctx", axis_index_groups=pairs, tiled=True)

    far = jnp.arange(FARS, dtype=jnp.int32)
    turned = (far < FARS // 2).astype(jnp.int32)
    own_turned = (rank < FARS // 2 * LINE).astype(jnp.int32)
    lane = (rank // LOWS % 2) ^ own_turned
    shard = far * LINE + (lane ^ turned) * LOWS + rank % LOWS
    limits = cache_length[0] - shard * slots

    kept = 2 * entries * FARS
    partial = pl.pallas_call(
        cache_kernel,
        out_shape=jax.ShapeDtypeStruct((LINE, head_dim + kept + STAT_ROWS, tokens), jnp.bfloat16),
        in_specs=[SMEM, VMEM, VMEM],
        out_specs=VMEM,
        scratch_shapes=[
            pltpu.VMEM((head_dim, FARS * slots), jnp.bfloat16),
            pltpu.VMEM((LINE // 2, FARS * slots, 2 * tokens), jnp.float32),
            pltpu.VMEM((LINE // 2, FARS * slots, 2 * tokens), jnp.bfloat16),
        ],
        compiler_params=SMALL,
        cost_estimate=pl.CostEstimate(
            flops=4 * LINE * tokens * head_dim * FARS * slots,
            bytes_accessed=1 << 20,
            transcendentals=LINE * tokens * FARS * slots,
        ),
        name="cache_term",
    )(limits, queries, cache)
    received = lax.all_to_all(partial, "ctx", 0, 0, axis_index_groups=NEARS, tiled=True)
    gain = jnp.broadcast_to(key_gain[:, None], (head_dim, tokens))
    return pl.pallas_call(
        final_kernel,
        out_shape=jax.ShapeDtypeStruct((tokens, head_dim), jnp.bfloat16),
        in_specs=[VMEM] * 5,
        out_specs=VMEM,
        compiler_params=SMALL,
        name="final_join",
    )(own_query, received, gain, cosine, sine)


def solution(mesh):
    return jax.shard_map(
        per_device,
        mesh=mesh,
        in_specs=(
            P("req", None),
            P(None, "ctx"),
            P(None, "ctx"),
            P(None, "ctx"),
            P(),
            P(),
            P(("req", "ctx"), None),
            P(("req", "ctx"), None),
            P("req"),
            P("req"),
        ),
        out_specs=P("req", "ctx"),
        check_vma=False,
    )
```

time: 89.9 us -> 68.3 us (0.76)
  waiting for transfers between devices: 14.9 us -> 2.34 us
  blocking collectives: 30.9 us -> 39.7 us
  starting transfers between devices: 23.3 us -> 15.3 us
  local copies, waits for them, and re-layouts: 5.02 us -> 1.4 us
  other arithmetic: 3.37 us -> 0.23 us
  matrix products: 2.35 us -> 0 us
    all_to_all x0 -> x1, blocking collectives: none -> 16 us  [per_device(): lax.all_to_all(partial, 'ctx', 0, 0, axis_index_groups=NEARS, tiled=True)]
    all_to_all x3 -> x1, waiting for transfers between devices: 14.9 us -> 2.34 us  [per_device(): lax.all_to_all(packed, 'ctx', 0, 0, axis_index_groups=LINES, tiled=True)]
    all_to_all x3 -> x1, starting transfers between devices: 23.3 us -> 15.3 us  [per_device(): lax.all_to_all(packed, 'ctx', 0, 0, axis_index_groups=LINES, tiled=True)]
    all_gather x1 -> x3, blocking collectives: 30.9 us -> 23.7 us  [per_device(): lax.all_gather(queries, 'ctx', axis_index_groups=pairs, tiled=True)]
    dot_general x3 -> x0, matrix products: 2.35 us -> none  [the longest x1 1.35 us: per_device(): lax.dot_general(key_projection_weight, hidden, weights, preferred_element...]
    unnamed x22 -> x8, local copies, waits for them, and re-layouts: 3.26 us -> 1.33 us
    another operation x2 -> x0, other arithmetic: 1.43 us -> none  [the longest x1 0.84 us: per_device(): jnp.stack([stored_cache_keys.reshape(slots, kv_heads, head_dim).transpose...]
    pallas_call x1 -> x3, Pallas kernels: 6.08 us -> 6.32 us  [the longest x1 3.3 us: per_device(): pl.pallas_call(pack_kernel, out_shape=jax.ShapeDtypeStruct((FARS, 2 * slo...]
  transfers between devices with their start and end apart: 3 -> 1, of which waited for: 2 -> 1; matrix products, arithmetic and copies ran while one was open for 6% -> 0% of each run, Pallas kernels for 0% -> 1%
where the time goes in v2:
time: 68.3 us; the launch traced here: 68 us
  blocking collectives  39.7 us (58%)
  starting transfers between devices  15.3 us (22%)
  Pallas kernels  7.57 us (11%)
  waiting for transfers between devices  2.34 us (3%)
  local copies, waits for them, and re-layouts  1.4 us (2%)
  between operations  1.4 us (2%)
    all_gather x3, blocking collectives, per_device(): lax.all_gather(queries, 'ctx', axis_index_groups=pairs, tiled=True)  23.7 us
    all_to_all x1, blocking collectives, per_device(): lax.all_to_all(partial, 'ctx', 0, 0, axis_index_groups=NEARS, tiled=True)  16 us
    all_to_all x1, starting transfers between devices, per_device(): lax.all_to_all(packed, 'ctx', 0, 0, axis_index_groups=LINES, tiled=True)  15.3 us
    pallas_call x1, Pallas kernels, per_device(): pl.pallas_call(pack_kernel, out_shape=jax.ShapeDtypeStruct((FARS, 2 * slo...  3.3 us
    pallas_call x1, Pallas kernels, per_device(): pl.pallas_call(cache_kernel, out_shape=jax.ShapeDtypeStruct((LINE, head_d...  2.38 us
    all_to_all x1, waiting for transfers between devices, per_device(): lax.all_to_all(packed, 'ctx', 0, 0, axis_index_groups=LINES, tiled=True)  2.34 us
  transfers between devices with their start and end apart: 1, of which 1 were waited for; matrix products, arithmetic and copies ran while one was open for 0% of the time, Pallas kernels for 1%

profile of v2, /device:TPU:1, one launch (start us, length us, event | category | flops | bytes accessed | tf_op | source)
XLA Modules:
  0.0 68.0 jit_solution(13795015979489063093)
XLA Ops:
  0.0 3.3 %pack.1 = bf16[8,264,128]{2,1,0:T(8,128)(2,1)} custom-call(bf16[128,5120]{1,0:T(8,128)(2,1)} %hidden_hbm.1, bf16[16,5120]{1,0:T(8,128)(2,1)} %bitcast.9, bf16[16,5120]{1,0:T(8,128)(2,1)} %bitcast.10, bf16[128,1024]{1,0:T(8,128)(2,1)} %keys_hbm.1, bf16[128,1024]{1,0:T(8,128)(2,1)} %values_hbm.1), custom_call_target="tpu_custom_call" | custom-call | flops 67108864 | bytes 4194304 | tf_op jit(solution)/shard_map/pack/pallas_call | solution.py:254
  3.3 0.0 copy-start
  3.3 0.0 copy-start.2
  3.3 15.3 %all-to-all-start = ((bf16[8,264,128]{2,1,0:T(8,128)(2,1)}), bf16[8,264,128]{2,1,0:T(8,128)(2,1)S(1)}, u32[]{:S(2)}, u32[]{:S(2)}) async-start(bf16[8,264,128]{2,1,0:T(8,128)(2,1)} %pack.1), calls=%async_computation | async-start | bytes 1081344 | tf_op jit(solution)/shard_map/all_to_all | solution.py:281
  20.0 0.2 multiply_sine_fusion
  20.2 0.0 copy-done
  20.2 0.0 copy-done.2
  20.2 0.0 copy-start.1
  20.2 1.3 %copy-done.1 = bf16[5120,128]{1,0:T(8,128)(2,1)S(1)} copy-done((bf16[5120,128]{1,0:T(8,128)(2,1)S(1)}, bf16[5120,128]{1,0:T(8,128)(2,1)}, u32[]{:S(2)}) %copy-start.1) | copy-done | bytes 1310744
  21.6 0.6 query.1.query_ref
  22.2 2.5 %all-gather = bf16[256,128]{1,0:T(8,128)(2,1)S(1)} all-gather(bf16[128,128]{1,0:T(8,128)(2,1)S(1)} %query.1.query_ref), channel_id=2, replica_groups={{0,8},{16,24},{32,40},{48,56},{64,72},{80,88},{96,104},{112,120},{128,1..., dimensions={0}, use_global_device_ids=true | all-gather | bytes 98304 | tf_op jit(solution)/shard_map/all_gather | solution.py:295
  24.7 5.6 %all_gather.10 = bf16[4,128,128]{2,1,0:T(8,128)(2,1)S(1)} all-gather(bf16[2,128,128]{2,1,0:T(8,128)(2,1)S(1)} %bitcast.8), channel_id=1, replica_groups={{0,16},{8,24},{32,48},{40,56},{64,80},{72,88},{96,112},{104,120},{128,1..., dimensions={0}, use_global_device_ids=true | all-gather | bytes 196608 | tf_op jit(solution)/shard_map/all_gather | solution.py:295
  30.2 15.7 %all_gather.11.queries_ref = bf16[8,128,128]{2,1,0:T(8,128)(2,1)S(1)} all-gather(bf16[4,128,128]{2,1,0:T(8,128)(2,1)S(1)} %all_gather.10), channel_id=1, replica_groups={{32,0},{40,8},{48,16},{56,24},{96,64},{104,72},{112,80},{120,88},{160,1..., dimensions={0}, use_global_device_ids=true | all-gather | bytes 393216 | tf_op jit(solution)/shard_map/all_gather | solution.py:295
  45.9 0.0 copy-start.3
  45.9 2.3 %all-to-all-done.cache_ref = bf16[8,264,128]{2,1,0:T(8,128)(2,1)S(1)} async-done(((bf16[8,264,128]{2,1,0:T(8,128)(2,1)}), bf16[8,264,128]{2,1,0:T(8,128)(2,1)S(1)}, u32[]{:S(2)}, u32[]{:S(2)}) %all-to-all-start) | async-done | bytes 540704 | tf_op jit(solution)/shard_map/all_to_all | solution.py:281
  48.2 2.4 %cache_term.1 = bf16[8,168,128]{2,1,0:T(8,128)(2,1)S(1)} custom-call(s32[8]{0:T(128)S(1)} %multiply_subtract_fusion.limit_ref, bf16[8,128,128]{2,1,0:T(8,128)(2,1)S(1)} %all_gather.11.queries_ref, bf16[8,264,128]{2,1,0:T(8,128)(2,1)S(1)} %all-to-all-done.cache_ref), custom_call_target="tpu_custom_call" | custom-call | flops 536870912 | bytes 1048576 | tf_op jit(solution)/shard_map/cache_term/pallas_call | solution.py:305
  50.6 16.0 %all_to_all.10.received_ref = bf16[8,168,128]{2,1,0:T(8,128)(2,1)S(1)} all-to-all(bf16[8,168,128]{2,1,0:T(8,128)(2,1)S(1)} %cache_term.1), channel_id=1, replica_groups={{32,40,48,56,0,8,16,24},{96,104,112,120,64,72,80,88},{160,168,176,184,1..., dimensions={0} | all-to-all | bytes 688128 | tf_op jit(solution)/shard_map/all_to_all | solution.py:323
  66.7 0.0 copy-done.3
  66.7 0.1 broadcast_in_dim.16.gain_ref
  66.7 1.3 %final_join.1 = bf16[128,128]{1,0:T(8,128)(2,1)} custom-call(bf16[128,128]{1,0:T(8,128)(2,1)S(1)} %query.1.query_ref, bf16[8,168,128]{2,1,0:T(8,128)(2,1)S(1)} %all_to_all.10.received_ref, f32[128,128]{1,0:T(8,128)S(1)} %broadcast_in_dim.16.gain_ref, f32[128,128]{1,0:T(8,128)S(1)} %get-tuple-element.7.cosine_ref, f32[128,128]{1,0:T(8,128)S(1)} %get-tuple-element.8.sine_ref), custom_call_target="tpu_custom_call" | custom-call | tf_op jit(solution)/shard_map/final_join/pallas_call | solution.py:325
  (4 shorter events, 0.0 us)
Async XLA Ops:
  3.3 16.9 %copy-start = (bf16[128,5120]{1,0:T(8,128)(2,1)S(1)}, bf16[128,5120]{1,0:T(8,128)(2,1)}, u32[]{:S(2)}) copy-start(bf16[128,5120]{1,0:T(8,128)(2,1)} %hidden_hbm.1) | copy-start | bytes 3932164
  3.3 16.9 %copy-start.2 = (f32[128]{0:T(128)S(1)}, f32[128]{0:T(128)}, u32[]{:S(2)}) copy-start(f32[128]{0:T(128)} %param.14) | copy-start | bytes 1540
  3.3 44.9 %all-to-all-start = ((bf16[8,264,128]{2,1,0:T(8,128)(2,1)}), bf16[8,264,128]{2,1,0:T(8,128)(2,1)S(1)}, u32[]{:S(2)}, u32[]{:S(2)}) async-start(bf16[8,264,128]{2,1,0:T(8,128)(2,1)} %pack.1), calls=%async_computation | async-start | bytes 1081344 | tf_op jit(solution)/shard_map/all_to_all | solution.py:281
  20.2 1.3 %copy-start.1 = (bf16[5120,128]{1,0:T(8,128)(2,1)S(1)}, bf16[5120,128]{1,0:T(8,128)(2,1)}, u32[]{:S(2)}) copy-start(bf16[5120,128]{1,0:T(8,128)(2,1)} %weight_ref.1) | copy-start | bytes 3932164
  45.9 20.8 %copy-start.3 = (f32[128]{0:T(128)S(1)}, f32[128]{0:T(128)}, u32[]{:S(2)}) copy-start(f32[128]{0:T(128)} %param.15) | copy-start | bytes 1540

commit v3 on v2

--- a/solution.py
+++ b/solution.py
@@ -14,6 +14,7 @@
 FLOOR = -1e29
 PART_ROWS = 8
 STAT_ROWS = 8
+HIDDEN_CHUNKS = 4
 
 
 def side_of(lane, far):
@@ -24,9 +25,8 @@
     return far * LINE + side_of(lane, far) * LOWS + low
 
 
-LINES = [
-    [rank_of(far, lane, low) for far in range(FARS)] for lane in range(2) for low in range(LOWS)
-]
+ORDER = (0, 4, 1, 5, 2, 6, 3, 7)
+LINES = [[rank_of(far, lane, low) for far in ORDER] for lane in range(2) for low in range(LOWS)]
 NEARS = [
     [rank_of(far, lane, low) for lane in range(2) for low in range(LOWS)] for far in range(FARS)
 ]
@@ -51,63 +51,78 @@
     values_hbm,
     out_hbm,
     hidden_ref,
-    key_weight_ref,
-    value_weight_ref,
-    keys_ref,
-    values_ref,
+    weight_ref,
+    cache_ref,
     part_ref,
-    in_sems,
-    key_sems,
-    value_sems,
+    hidden_sems,
+    weight_sems,
+    cache_sems,
+    store_sems,
     part_sems,
 ):
-    slots = keys_ref.shape[0]
-    head_dim = keys_ref.shape[1] // FARS
-    loads = [
-        pltpu.make_async_copy(source, target, in_sems.at[k])
-        for k, (source, target) in enumerate(
-            (
-                (keys_hbm, keys_ref),
-                (values_hbm, values_ref),
-                (hidden_hbm, hidden_ref),
-                (key_weight_hbm, key_weight_ref),
-                (value_weight_hbm, value_weight_ref),
-            )
+    slots = keys_hbm.shape[0]
+    head_dim = keys_hbm.shape[1] // FARS
+    columns = key_weight_hbm.shape[0]
+    depth = hidden_hbm.shape[1] // HIDDEN_CHUNKS
+    cache_loads = [
+        pltpu.make_async_copy(source, cache_ref.at[k], cache_sems.at[k])
+        for k, source in enumerate((keys_hbm, values_hbm))
+    ]
+    weight_loads = [
+        pltpu.make_async_copy(
+            source, weight_ref.at[pl.ds(k * columns, columns), :], weight_sems.at[k]
         )
+        for k, source in enumerate((key_weight_hbm, value_weight_hbm))
     ]
-    for load in loads:
+    hidden_loads = [
+        pltpu.make_async_copy(
+            hidden_hbm.at[:, pl.ds(k * depth, depth)],
+            hidden_ref.at[:, pl.ds(k * depth, depth)],
+            hidden_sems.at[k],
+        )
+        for k in range(HIDDEN_CHUNKS)
+    ]
+    for load in weight_loads + hidden_loads[:2] + cache_loads + hidden_loads[2:]:
         load.start()
-    stores = []
-    for k, (ref, sems) in enumerate(((keys_ref, key_sems), (values_ref, value_sems))):
-        loads[k].wait()
-        for far in range(FARS):
-            store = pltpu.make_async_copy(
-                ref.at[:, pl.ds(far * head_dim, head_dim)],
-                out_hbm.at[far, pl.ds(k * slots, slots), :],
-                sems.at[far],
-            )
-            store.start()
-            stores.append(store)
-    for load in loads[2:]:
+    entries = columns // FARS
+    shape = (FARS * PART_ROWS, 2 * columns)
+    target = lax.broadcasted_iota(jnp.int32, shape, 0)
+    source = lax.broadcasted_iota(jnp.int32, shape, 1)
+    inside = target % PART_ROWS
+    pick = (inside < 2 * entries) & (source == inside * FARS + target // PART_ROWS)
+    pick = pick.astype(jnp.bfloat16)
+    for load in weight_loads:
         load.wait()
     across = (((1,), (1,)), ((), ()))
-    key_part, value_part = [
-        lax.dot_general(ref[...], hidden_ref[...], across, preferred_element_type=jnp.float32)
-        for ref in (key_weight_ref, value_weight_ref)
-    ]
-    entries = key_part.shape[0] // FARS
-    rows = jnp.concatenate([key_part, value_part], axis=0)
-    target = lax.broadcasted_iota(jnp.int32, (FARS * PART_ROWS, rows.shape[0]), 0)
-    source = lax.broadcasted_iota(jnp.int32, (FARS * PART_ROWS, rows.shape[0]), 1)
-    inside = target % PART_ROWS
-    pick = (inside < 2 * entries) & (source == inside * FARS + target // PART_ROWS)
+    stores = []
+    total = None
+    for k in range(HIDDEN_CHUNKS):
+        hidden_loads[k].wait()
+        block = slice(k * depth, (k + 1) * depth)
+        term = lax.dot_general(
+            hidden_ref[:, block], weight_ref[:, block], across, preferred_element_type=jnp.float32
+        )
+        total = term if total is None else total + term
+        if k == 1:
+            for kind, load in enumerate(cache_loads):
+                load.wait()
+                for far in range(FARS):
+                    store = pltpu.make_async_copy(
+                        cache_ref.at[kind, :, pl.ds(far * head_dim, head_dim)],
+                        out_hbm.at[ORDER.index(far), pl.ds(kind * slots, slots), :],
+                        store_sems.at[kind, far],
+                    )
+                    store.start()
+                    stores.append(store)
     ordered = jnp.dot(
-        pick.astype(jnp.bfloat16), rows.astype(jnp.bfloat16), preferred_element_type=jnp.float32
+        pick, total.T.astype(jnp.bfloat16), preferred_element_type=jnp.float32
     ).astype(jnp.bfloat16)
     for far in range(FARS):
         part_ref[far] = ordered[far * PART_ROWS : (far + 1) * PART_ROWS]
         store = pltpu.make_async_copy(
-            part_ref.at[far], out_hbm.at[far, pl.ds(2 * slots, PART_ROWS), :], part_sems.at[far]
+            part_ref.at[far],
+            out_hbm.at[ORDER.index(far), pl.ds(2 * slots, PART_ROWS), :],
+            part_sems.at[far],
         )
         store.start()
         stores.append(store)
@@ -125,7 +140,9 @@
         turned_ref[:, far * slots : (far + 1) * slots] = cache_ref[far, slots : 2 * slots].T
     slot = lax.broadcasted_iota(jnp.int32, (slots, wide), 0)
 
-    rows = jnp.concatenate([cache_ref[far, 2 * slots :] for far in range(FARS)], axis=0)
+    rows = jnp.concatenate(
+        [cache_ref[ORDER.index(far), 2 * slots :] for far in range(FARS)], axis=0
+    )
     entries = head_dim // (FARS * LINE)
     kept = 2 * entries * FARS
     target = lax.broadcasted_iota(jnp.int32, (kept, FARS * PART_ROWS), 0)
@@ -258,14 +275,13 @@
         out_specs=HBM,
         scratch_shapes=[
             pltpu.VMEM(hidden.shape, jnp.bfloat16),
-            pltpu.VMEM(key_projection_weight.shape[::-1], jnp.bfloat16),
-            pltpu.VMEM(value_projection_weight.shape[::-1], jnp.bfloat16),
-            pltpu.VMEM(stored_cache_keys.shape, jnp.bfloat16),
-            pltpu.VMEM(stored_cache_values.shape, jnp.bfloat16),
+            pltpu.VMEM((2 * key_projection_weight.shape[1], hidden.shape[1]), jnp.bfloat16),
+            pltpu.VMEM((2, *stored_cache_keys.shape), jnp.bfloat16),
             pltpu.VMEM((FARS, PART_ROWS, tokens), jnp.bfloat16),
-            pltpu.SemaphoreType.DMA((5,)),
-            pltpu.SemaphoreType.DMA((FARS,)),
-            pltpu.SemaphoreType.DMA((FARS,)),
+            pltpu.SemaphoreType.DMA((HIDDEN_CHUNKS,)),
+            pltpu.SemaphoreType.DMA((2,)),
+            pltpu.SemaphoreType.DMA((2,)),
+            pltpu.SemaphoreType.DMA((2, FARS)),
             pltpu.SemaphoreType.DMA((FARS,)),
         ],
         compiler_params=WHOLE,
@@ -294,7 +310,7 @@
     for pairs in (CORE_PAIRS, ROW_PAIRS, LANE_PAIRS):
         queries = lax.all_gather(queries, "ctx", axis_index_groups=pairs, tiled=True)
 
-    far = jnp.arange(FARS, dtype=jnp.int32)
+    far = jnp.array(ORDER, jnp.int32)
     turned = (far < FARS // 2).astype(jnp.int32)
     own_turned = (rank < FARS // 2 * LINE).astype(jnp.int32)
     lane = (rank // LOWS % 2) ^ own_turned

time: 68.3 us -> 64.9 us (0.950)
  blocking collectives: 39.7 us -> 33 us
  waiting for transfers between devices: 2.34 us -> 5.22 us
    all_gather x3, blocking collectives: 23.7 us -> 19.2 us  [per_device(): lax.all_gather(queries, 'ctx', axis_index_groups=pairs, tiled=True)]
    all_to_all x1, waiting for transfers between devices: 2.34 us -> 5.22 us  [per_device(): lax.all_to_all(packed, 'ctx', 0, 0, axis_index_groups=LINES, tiled=True)]
    all_to_all x1, blocking collectives: 16 us -> 13.8 us  [per_device(): lax.all_to_all(partial, 'ctx', 0, 0, axis_index_groups=NEARS, tiled=True)]
where the time goes in v3:
time: 64.9 us; the launch traced here: 64.2 us
  blocking collectives  33 us (51%)
  starting transfers between devices  15.3 us (24%)
  Pallas kernels  7.62 us (12%)
  waiting for transfers between devices  5.22 us (8%)
  local copies, waits for them, and re-layouts  1.41 us (2%)
  between operations  1.41 us (2%)
    all_gather x3, blocking collectives, per_device(): lax.all_gather(queries, 'ctx', axis_index_groups=pairs, tiled=True)  19.2 us
    all_to_all x1, starting transfers between devices, per_device(): lax.all_to_all(packed, 'ctx', 0, 0, axis_index_groups=LINES, tiled=True)  15.3 us
    all_to_all x1, blocking collectives, per_device(): lax.all_to_all(partial, 'ctx', 0, 0, axis_index_groups=NEARS, tiled=True)  13.8 us
    all_to_all x1, waiting for transfers between devices, per_device(): lax.all_to_all(packed, 'ctx', 0, 0, axis_index_groups=LINES, tiled=True)  5.22 us
    pallas_call x1, Pallas kernels, per_device(): pl.pallas_call(pack_kernel, out_shape=jax.ShapeDtypeStruct((FARS, 2 * slo...  3.34 us
    pallas_call x1, Pallas kernels, per_device(): pl.pallas_call(cache_kernel, out_shape=jax.ShapeDtypeStruct((LINE, head_d...  2.38 us
    unnamed x12, local copies, waits for them, and re-layouts  1.34 us
  transfers between devices with their start and end apart: 1, of which 1 were waited for; matrix products, arithmetic and copies ran while one was open for 0% of the time, Pallas kernels for 1%

profile of v3, /device:TPU:1, one launch (start us, length us, event | category | flops | bytes accessed | tf_op | source)
XLA Modules:
  0.0 64.2 jit_solution(4425618929324385021)
XLA Ops:
  0.0 3.3 %pack.1 = bf16[8,264,128]{2,1,0:T(8,128)(2,1)} custom-call(bf16[128,5120]{1,0:T(8,128)(2,1)} %hidden_hbm.1, bf16[16,5120]{1,0:T(8,128)(2,1)} %bitcast.9, bf16[16,5120]{1,0:T(8,128)(2,1)} %bitcast.10, bf16[128,1024]{1,0:T(8,128)(2,1)} %keys_hbm.1, bf16[128,1024]{1,0:T(8,128)(2,1)} %values_hbm.1), custom_call_target="tpu_custom_call" | custom-call | flops 67108864 | bytes 4194304 | tf_op jit(solution)/shard_map/pack/pallas_call | solution.py:271
  3.4 0.0 copy-start
  3.4 0.0 copy-start.2
  3.4 15.3 %all-to-all-start = ((bf16[8,264,128]{2,1,0:T(8,128)(2,1)}), bf16[8,264,128]{2,1,0:T(8,128)(2,1)S(1)}, u32[]{:S(2)}, u32[]{:S(2)}) async-start(bf16[8,264,128]{2,1,0:T(8,128)(2,1)} %pack.1), calls=%async_computation | async-start | bytes 1081344 | tf_op jit(solution)/shard_map/all_to_all | solution.py:297
  20.0 0.2 multiply_sine_fusion
  20.3 0.0 copy-done
  20.3 0.0 copy-done.2
  20.3 0.0 copy-start.1
  20.3 1.3 %copy-done.1 = bf16[5120,128]{1,0:T(8,128)(2,1)S(1)} copy-done((bf16[5120,128]{1,0:T(8,128)(2,1)S(1)}, bf16[5120,128]{1,0:T(8,128)(2,1)}, u32[]{:S(2)}) %copy-start.1) | copy-done | bytes 1310744
  21.6 0.0 copy-start.4
  21.6 0.0 copy-start.5
  21.6 0.6 %query.1.query_ref = bf16[128,128]{1,0:T(8,128)(2,1)S(1)} custom-call(bf16[128,5120]{1,0:T(8,128)(2,1)S(1)} %copy-done, bf16[5120,128]{1,0:T(8,128)(2,1)S(1)} %copy-done.1, f32[1,128]{1,0:T(1,128)S(1)} %bitcast.7, f32[128,128]{1,0:T(8,128)S(1)} %get-tuple-element.7.cosine_ref, f32[128,128]{1,0:T(8,128)S(1)} %get-tuple-element.8.sine_ref), custom_call_target="tpu_custom_call" | custom-call | flops 268435456 | bytes 2097152 | tf_op jit(solution)/shard_map/query/pallas_call | solution.py:300
  22.3 2.5 %all-gather = bf16[256,128]{1,0:T(8,128)(2,1)S(1)} all-gather(bf16[128,128]{1,0:T(8,128)(2,1)S(1)} %query.1.query_ref), channel_id=2, replica_groups={{0,8},{16,24},{32,40},{48,56},{64,72},{80,88},{96,104},{112,120},{128,1..., dimensions={0}, use_global_device_ids=true | all-gather | bytes 98304 | tf_op jit(solution)/shard_map/all_gather | solution.py:311
  24.7 5.3 %all_gather.10 = bf16[4,128,128]{2,1,0:T(8,128)(2,1)S(1)} all-gather(bf16[2,128,128]{2,1,0:T(8,128)(2,1)S(1)} %bitcast.8), channel_id=1, replica_groups={{0,16},{8,24},{32,48},{40,56},{64,80},{72,88},{96,112},{104,120},{128,1..., dimensions={0}, use_global_device_ids=true | all-gather | bytes 196608 | tf_op jit(solution)/shard_map/all_gather | solution.py:311
  30.0 11.4 %all_gather.11.queries_ref = bf16[8,128,128]{2,1,0:T(8,128)(2,1)S(1)} all-gather(bf16[4,128,128]{2,1,0:T(8,128)(2,1)S(1)} %all_gather.10), channel_id=1, replica_groups={{32,0},{40,8},{48,16},{56,24},{96,64},{104,72},{112,80},{120,88},{160,1..., dimensions={0}, use_global_device_ids=true | all-gather | bytes 393216 | tf_op jit(solution)/shard_map/all_gather | solution.py:311
  41.4 0.0 copy-done.4
  41.4 0.0 copy-done.5
  41.4 0.0 copy-start.3
  41.4 5.2 %all-to-all-done.cache_ref = bf16[8,264,128]{2,1,0:T(8,128)(2,1)S(1)} async-done(((bf16[8,264,128]{2,1,0:T(8,128)(2,1)}), bf16[8,264,128]{2,1,0:T(8,128)(2,1)S(1)}, u32[]{:S(2)}, u32[]{:S(2)}) %all-to-all-start) | async-done | bytes 540704 | tf_op jit(solution)/shard_map/all_to_all | solution.py:297
  46.6 2.4 %cache_term.1 = bf16[8,168,128]{2,1,0:T(8,128)(2,1)S(1)} custom-call(s32[8]{0:T(128)S(1)} %fusion.1.limit_ref, bf16[8,128,128]{2,1,0:T(8,128)(2,1)S(1)} %all_gather.11.queries_ref, bf16[8,264,128]{2,1,0:T(8,128)(2,1)S(1)} %all-to-all-done.cache_ref), custom_call_target="tpu_custom_call" | custom-call | flops 536870912 | bytes 1048576 | tf_op jit(solution)/shard_map/cache_term/pallas_call | solution.py:321
  49.0 13.8 %all_to_all.10.received_ref = bf16[8,168,128]{2,1,0:T(8,128)(2,1)S(1)} all-to-all(bf16[8,168,128]{2,1,0:T(8,128)(2,1)S(1)} %cache_term.1), channel_id=1, replica_groups={{32,40,48,56,0,8,16,24},{96,104,112,120,64,72,80,88},{160,168,176,184,1..., dimensions={0} | all-to-all | bytes 688128 | tf_op jit(solution)/shard_map/all_to_all | solution.py:339
  62.9 0.0 copy-done.3
  62.9 0.1 broadcast_in_dim.16.gain_ref
  62.9 1.3 %final_join.1 = bf16[128,128]{1,0:T(8,128)(2,1)} custom-call(bf16[128,128]{1,0:T(8,128)(2,1)S(1)} %query.1.query_ref, bf16[8,168,128]{2,1,0:T(8,128)(2,1)S(1)} %all_to_all.10.received_ref, f32[128,128]{1,0:T(8,128)S(1)} %broadcast_in_dim.16.gain_ref, f32[128,128]{1,0:T(8,128)S(1)} %get-tuple-element.7.cosine_ref, f32[128,128]{1,0:T(8,128)S(1)} %get-tuple-element.8.sine_ref), custom_call_target="tpu_custom_call" | custom-call | tf_op jit(solution)/shard_map/final_join/pallas_call | solution.py:341
  (4 shorter events, 0.0 us)
Async XLA Ops:
  3.4 16.9 %copy-start = (bf16[128,5120]{1,0:T(8,128)(2,1)S(1)}, bf16[128,5120]{1,0:T(8,128)(2,1)}, u32[]{:S(2)}) copy-start(bf16[128,5120]{1,0:T(8,128)(2,1)} %hidden_hbm.1) | copy-start | bytes 3932164
  3.4 16.9 %copy-start.2 = (f32[128]{0:T(128)S(1)}, f32[128]{0:T(128)}, u32[]{:S(2)}) copy-start(f32[128]{0:T(128)} %param.15) | copy-start | bytes 1540
  3.4 43.3 %all-to-all-start = ((bf16[8,264,128]{2,1,0:T(8,128)(2,1)}), bf16[8,264,128]{2,1,0:T(8,128)(2,1)S(1)}, u32[]{:S(2)}, u32[]{:S(2)}) async-start(bf16[8,264,128]{2,1,0:T(8,128)(2,1)} %pack.1), calls=%async_computation | async-start | bytes 1081344 | tf_op jit(solution)/shard_map/all_to_all | solution.py:297
  20.3 1.3 %copy-start.1 = (bf16[5120,128]{1,0:T(8,128)(2,1)S(1)}, bf16[5120,128]{1,0:T(8,128)(2,1)}, u32[]{:S(2)}) copy-start(bf16[5120,128]{1,0:T(8,128)(2,1)} %weight_ref.1) | copy-start | bytes 3932164
  21.6 19.8 %copy-start.4 = (s32[8]{0:T(128)S(1)}, s32[8]{0:T(128)}, u32[]{:S(2)}) copy-start(s32[8]{0:T(128)} %constant.58) | copy-start | bytes 100
  21.6 19.8 %copy-start.5 = (s32[8]{0:T(128)S(1)}, s32[8]{0:T(128)}, u32[]{:S(2)}) copy-start(s32[8]{0:T(128)} %constant.60) | copy-start | bytes 100
  41.4 21.4 %copy-start.3 = (f32[128]{0:T(128)S(1)}, f32[128]{0:T(128)}, u32[]{:S(2)}) copy-start(f32[128]{0:T(128)} %param.16) | copy-start | bytes 1540
